TPU v7x, 32 devices: a whole 2x2x4 slice. The times are simulated.
32 devices in a mesh: snap: 2 (over core), shard: 16 (over z, y, x).
Axes of the slice: x: 2, y: 2, z: 4, core: 2. Of those that a mesh axis runs over, the one named last changes fastest.
Arguments:
- snapshots: float32 [32, 524288], P(('snap', 'shard')), may hold values from -6 to 6
- coefficients: float32 [32], P(('snap', 'shard')), may hold values from -1 to 1
Outputs:
- synthesized: float32 [524288], P('shard')
All inputs are finite; a program needn't handle non-finite values.
Results may differ from a plain program's by a relative error of at most 0.000078.
Values sent between devices are 32-bit elements; how exact they have to be, the bound alone decides.
No kernel may reach another device: no remote copies, remote signals or barrier semaphores. Data moves between devices by JAX's collectives and lax.ppermute only.
A program may use at most 64 MiB of HBM per device.

v0:
```python
import jax
import jax.numpy as jnp
from jax import lax
from jax.sharding import PartitionSpec as P


def per_device(snapshots, coefficients):
    partial_value = lax.psum_scatter(
        jnp.sum(coefficients[:, None] * snapshots, axis=0), "shard", scatter_dimension=0, tiled=True
    )
    return lax.psum(partial_value, "snap")


def solution(mesh):
    in_specs = (P(("snap", "shard"), None), P(("snap", "shard")))
    out_specs = P("shard")
    return jax.shard_map(
        per_device, mesh=mesh, in_specs=in_specs, out_specs=out_specs, check_vma=False
    )
```

profile of v0, /device:TPU:0, one launch (start us, length us, event | category | flops | bytes accessed | tf_op | source)
XLA Modules:
  0.0 170.1 jit_solution(14000131802462258670)
XLA Ops:
  6.5 0.0 all-reduce.6.cloned.1.call-start
  7.2 4.4 %broadcast_multiply_fusion = f32[1,524288]{1,0:T(1,128)} fusion(f32[1,524288]{1,0:T(1,128)} %param.2, f32[]{:T(128)} %bitcast.3), kind=kLoop, calls=%fused_computation | loop fusion | flops 524288 | bytes 4194308 | tf_op jit(solution)/shard_map/mul | solution.py:9
  11.6 0.0 copy-start
  11.6 0.0 all-reduce.6.cloned.1.call-update
  11.7 0.0 all-reduce.4.cloned.1.call-start
  11.7 0.6 copy-done
  12.3 0.6 dynamic-slice
  13.5 128.7 %all-reduce.6.cloned.1.call-done = f32[524288]{0:T(1024)} async-done(((f32[524288]{0:T(1024)}), f32[524288]{0:T(1024)}) %all-reduce.6.cloned.1.call-update) | async-done | bytes 2097168
  142.2 1.6 dynamic-slice.1
  143.8 0.0 all-reduce.4.cloned.1.call-update
  143.8 17.9 %all-reduce.4.cloned.1.call-done = f32[32768]{0:T(1024)} async-done(((f32[32768]{0:T(1024)}), f32[32768]{0:T(1024)}) %all-reduce.4.cloned.1.call-update) | async-done | bytes 131088 | tf_op jit(solution)/shard_map/psum | solution.py:11
  161.7 1.6 copy.6
Async XLA Ops:
  6.5 135.6 %all-reduce.6.cloned.1.call-start = ((), (), s32[]{:S(2)}) async-start(), calls=%async_computation.1 | async-start | bytes 4194304
  11.6 0.7 copy-start
  11.7 150.0 %all-reduce.4.cloned.1.call-start = ((), (), s32[]{:S(2)}) async-start(), calls=%async_computation | async-start | bytes 262144 | tf_op jit(solution)/shard_map/psum | solution.py:11
Sparse Core Ops, SparseCore 0:
  12.8 129.3 all-reduce.5
  144.5 17.1 all-reduce.3
where the time goes:
time: 170 us
  waiting for transfers between devices  147 us (86%)
  between operations  14.7 us (9%)
  other arithmetic  4.44 us (3%)
  local copies, waits for them, and re-layouts  4.29 us (3%)
    unnamed x3, waiting for transfers between devices  129 us
    psum x1, waiting for transfers between devices, per_device(): return lax.psum(partial_value, 'snap')  17.9 us
    mul x1, other arithmetic, per_device(): coefficients[:, None] * snapshots  4.44 us
    unnamed x5, local copies, waits for them, and re-layouts  4.29 us
  transfers between devices with their start and end apart: 2, of which 2 were waited for; matrix products, arithmetic and copies ran while one was open for 0% of the time, Pallas kernels for 0%

commit v1 on v0

v1 whole, which is shorter than its diff:
```python
import jax
import jax.numpy as jnp
from jax import lax
from jax.experimental import pallas as pl
from jax.experimental.pallas import tpu as pltpu
from jax.sharding import PartitionSpec as P

LANES = 128


def span(masks):
    offsets = [0]
    for mask in masks:
        offsets = offsets + [offset ^ mask for offset in offsets]
    return offsets


def phases_of(bits):
    rest = [(1 << b,) for b in range(min(4, bits), bits)]
    if bits < 4:
        return [(1 << b,) for b in range(bits)], [(1 << b,) for b in range(bits)]
    return [(1,), (2, 4), (8,)] + rest, [(2,), (1, 4), (8,)] + rest


def offsets_of(phases):
    offsets = [0]
    for masks in phases:
        offsets = [a ^ b for a in offsets for b in span(masks)]
    return offsets


def scaled_half(source, scale, half, order, shard, offsets):
    blocks, inner, _, rows, lanes = source.shape

    def kernel(half_ref, order_ref, shard_ref, scale_ref, source_ref, out_ref, sems):
        copies = []
        for k, (even, odd) in enumerate(zip(*offsets)):
            block = shard_ref[0] ^ jnp.where(order_ref[0] == 0, even, odd)
            copy = pltpu.make_async_copy(source_ref.at[block, :, half_ref[0]], out_ref.at[k], sems.at[k])
            copy.start()
            copies.append(copy)
        factor = scale_ref[0]
        for k, copy in enumerate(copies):
            copy.wait()
            out_ref[k] = out_ref[k] * factor

    smem = pl.BlockSpec(memory_space=pltpu.SMEM)
    return pl.pallas_call(
        kernel,
        out_shape=pltpu.VMEM((blocks, inner, rows, lanes), jnp.float32),
        in_specs=[smem, smem, smem, smem, pl.BlockSpec(memory_space=pltpu.HBM)],
        out_specs=pl.BlockSpec(memory_space=pltpu.VMEM),
        scratch_shapes=[pltpu.SemaphoreType.DMA((blocks,))],
    )(half.reshape(1), order.reshape(1), shard.reshape(1), scale, source)


def solution(mesh):
    snaps, shards = mesh.shape["snap"], mesh.shape["shard"]
    bits = shards.bit_length() - 1
    snap_bits = snaps.bit_length() - 1
    phases = phases_of(bits)
    offsets = [offsets_of(p) for p in phases]

    def per_device(snapshots, coefficients):
        params = snapshots.shape[1]
        rows = params // shards // snaps // LANES
        snap, shard = lax.axis_index("snap"), lax.axis_index("shard")
        source = snapshots.reshape(shards, -1, 2, rows, LANES)
        mine = snap & 1
        send = scaled_half(source, coefficients, 1 - mine, 1 - mine, shard, offsets)
        got = lax.ppermute(send, "snap", [(s, s ^ 1) for s in range(snaps)])
        part = scaled_half(source, coefficients, mine, mine, shard, offsets) + got
        for bit in range(1, snap_bits):
            mine = (snap >> bit) & 1
            part = part.reshape(shards, -1, 2, rows, LANES)
            send = lax.dynamic_index_in_dim(part, 1 - mine, 2, keepdims=False)
            keep = lax.dynamic_index_in_dim(part, mine, 2, keepdims=False)
            part = keep + lax.ppermute(send, "snap", [(s, s ^ (1 << bit)) for s in range(snaps)])
        part = part.reshape(shards, rows, LANES)
        for even, odd in zip(*phases):
            masks = list(zip(span(even), span(odd)))
            part = part.reshape(len(masks), -1, rows, LANES)
            total = part[0]
            for k in reversed(range(1, len(masks))):
                pairs = [
                    (s * shards + d, s * shards + (d ^ masks[k][s & 1]))
                    for s in range(snaps) for d in range(shards)
                ]
                total = total + lax.ppermute(part[k], ("snap", "shard"), pairs)
            part = total
        own = part.reshape(rows, LANES)
        for bit in range(snap_bits):
            mine = (snap >> bit) & 1
            got = lax.ppermute(own, "snap", [(s, s ^ (1 << bit)) for s in range(snaps)])
            own = jnp.stack([jnp.where(mine == 0, own, got), jnp.where(mine == 0, got, own)])
        return own.reshape(-1)

    in_specs = (P(("snap", "shard"), None), P(("snap", "shard")))
    return jax.shard_map(per_device, mesh=mesh, in_specs=in_specs, out_specs=P("shard"), check_vma=False)
```

time: 170 us -> 31.8 us (0.19)
  waiting for transfers between devices: 147 us -> 17.1 us
  between operations: 14.7 us -> 0.73 us
  starting transfers between devices: 0.04 us -> 9.96 us
  local copies, waits for them, and re-layouts: 4.29 us -> 0.07 us
  other arithmetic: 4.44 us -> 0.92 us
  Pallas kernels: 0 us -> 2.76 us
    unnamed x3 -> x0, waiting for transfers between devices: 129 us -> none
    psum x1 -> x0, waiting for transfers between devices: 17.9 us -> none  [per_device(): return lax.psum(partial_value, 'snap')]
    ppermute x0 -> x7, waiting for transfers between devices: none -> 17.1 us  [the longest x5 15 us: per_device(): total = total + lax.ppermute(part[k], ('snap', 'shard'), pairs)]
    ppermute x0 -> x7, starting transfers between devices: none -> 9.96 us  [the longest x5 9.34 us: per_device(): total = total + lax.ppermute(part[k], ('snap', 'shard'), pairs)]
    mul x1 -> x0, other arithmetic: 4.44 us -> none  [per_device(): coefficients[:, None] * snapshots]
    unnamed x5 -> x0, local copies, waits for them, and re-layouts: 4.29 us -> none
    pallas_call x0 -> x2, Pallas kernels: none -> 2.76 us  [scaled_half(): pl.pallas_call(kernel, out_shape=pltpu.VMEM((blocks, inner, rows, lanes),...]
  transfers between devices with their start and end apart: 2 -> 7, of which waited for: 2 -> 6; matrix products, arithmetic and copies ran while one was open for 0% -> 0% of each run, Pallas kernels for 0% -> 4%
where the time goes in v1:
time: 31.8 us; the launch traced here: 31.6 us
  waiting for transfers between devices  17.1 us (54%)
  starting transfers between devices  9.96 us (31%)
  Pallas kernels  2.76 us (9%)
  other arithmetic  0.92 us (3%)
  between operations  0.73 us (2%)
    ppermute x5, waiting for transfers between devices, per_device(): total = total + lax.ppermute(part[k], ('snap', 'shard'), pairs)  15 us
    ppermute x5, starting transfers between devices, per_device(): total = total + lax.ppermute(part[k], ('snap', 'shard'), pairs)  9.34 us
    pallas_call x2, Pallas kernels, scaled_half(): pl.pallas_call(kernel, out_shape=pltpu.VMEM((blocks, inner, rows, lanes),...  2.76 us
    ppermute x1, waiting for transfers between devices, per_device(): got = lax.ppermute(own, 'snap', [(s, s ^ 1 << bit) for s in range(snaps)])  1.24 us
    ppermute x1, waiting for transfers between devices, per_device(): got = lax.ppermute(send, 'snap', [(s, s ^ 1) for s in range(snaps)])  0.9 us
    another operation x2, other arithmetic, per_device(): jnp.stack([jnp.where(mine == 0, own, got), jnp.where(mine == 0, got, own)])  0.68 us
  transfers between devices with their start and end apart: 7, of which 6 were waited for; matrix products, arithmetic and copies ran while one was open for 0% of the time, Pallas kernels for 4%

profile of v1, /device:TPU:0, one launch (start us, length us, event | category | flops | bytes accessed | tf_op | source)
XLA Modules:
  0.0 31.6 jit_solution(8739507764630973846)
XLA Ops:
  0.7 1.4 %shard_map.29 = f32[16,1,128,128]{3,2,1,0:T(8,128)S(1)} custom-call(s32[1]{0:T(128)} %bitcast.3.half_ref.order_ref, s32[1]{0:T(128)} %bitcast.3.half_ref.order_ref, s32[1]{0:T(128)} %bitcast.1.shard_ref, f32[1]{0:T(128)S(6)} %copy.4.scale_ref, f32[16,1,2,128,128]{4,3,2,1,0:T(8,128)} %bitcast.18), custom_call_target="tpu_custom_call" | custom-call | tf_op jit(solution)/shard_map/pallas_call | solution.py:48
  2.0 0.6 %collective-permute-start = (f32[16,1,128,128]{3,2,1,0:T(8,128)S(1)}, f32[16,1,128,128]{3,2,1,0:T(8,128)S(1)}, u32[]{:S(2)}, u32[]{:S(2)}) collective-permute-start(f32[16,1,128,128]{3,2,1,0:T(8,128)S(1)} %shard_map.29), channel_id=1, source_target_pairs={{0,16},{16,0},{1,17},{17,1},{2,18},{18,2},{3,19},{19,3},{4,20},{20... | collective-permute-start | bytes 3145736 | tf_op jit(solution)/shard_map/ppermute | solution.py:71
  2.6 1.4 %shard_map.28 = f32[16,1,128,128]{3,2,1,0:T(8,128)S(1)} custom-call(s32[1]{0:T(128)} %bitcast.half_ref.order_ref, s32[1]{0:T(128)} %bitcast.half_ref.order_ref, s32[1]{0:T(128)} %bitcast.1.shard_ref, f32[1]{0:T(128)S(6)} %copy.4.scale_ref, f32[16,1,2,128,128]{4,3,2,1,0:T(8,128)} %bitcast.19), custom_call_target="tpu_custom_call" | custom-call | tf_op jit(solution)/shard_map/pallas_call | solution.py:48
  4.0 0.9 %collective-permute-done = f32[16,1,128,128]{3,2,1,0:T(8,128)S(1)} collective-permute-done((f32[16,1,128,128]{3,2,1,0:T(8,128)S(1)}, f32[16,1,128,128]{3,2,1,0:T(8,128)S(1)}, u32[]{:S(2)}, u32[]{:S(2)}) %collective-permute-start) | collective-permute-done | bytes 1048608 | tf_op jit(solution)/shard_map/ppermute | solution.py:71
  4.9 0.1 add.18
  5.1 2.9 %collective-permute-start.1 = (f32[8,128,128]{2,1,0:T(8,128)S(1)}, f32[8,128,128]{2,1,0:T(8,128)S(1)}, u32[]{:S(2)}, u32[]{:S(2)}) collective-permute-start(f32[8,128,128]{2,1,0:T(8,128)S(1)} %slice_bitcast_fusion), channel_id=1, source_target_pairs={{0,1},{1,0},{2,3},{3,2},{4,5},{5,4},{6,7},{7,6},{8,9},{9,8},{10,11... | collective-permute-start | bytes 1572872 | tf_op jit(solution)/shard_map/ppermute | solution.py:89
  8.0 7.2 %collective-permute-done.1 = f32[8,128,128]{2,1,0:T(8,128)S(1)} collective-permute-done((f32[8,128,128]{2,1,0:T(8,128)S(1)}, f32[8,128,128]{2,1,0:T(8,128)S(1)}, u32[]{:S(2)}, u32[]{:S(2)}) %collective-permute-start.1) | collective-permute-done | bytes 524320 | tf_op jit(solution)/shard_map/ppermute | solution.py:89
  15.1 0.1 fusion
  15.3 3.1 %collective-permute-start.2 = (f32[2,128,128]{2,1,0:T(8,128)S(1)}, f32[2,128,128]{2,1,0:T(8,128)S(1)}, u32[]{:S(2)}, u32[]{:S(2)}) collective-permute-start(f32[2,128,128]{2,1,0:T(8,128)S(1)} %get-tuple-element.5), channel_id=1, source_target_pairs={{0,6},{1,7},{2,4},{3,5},{4,2},{5,3},{6,0},{7,1},{8,14},{9,15},{10,... | collective-permute-start | bytes 393224 | tf_op jit(solution)/shard_map/ppermute | solution.py:89
  18.4 0.4 %collective-permute-start.3 = (f32[2,128,128]{2,1,0:T(8,128)S(1)}, f32[2,128,128]{2,1,0:T(8,128)S(1)}, u32[]{:S(2)}, u32[]{:S(2)}) collective-permute-start(f32[2,128,128]{2,1,0:T(8,128)S(1)} %get-tuple-element.7), channel_id=1, source_target_pairs={{0,4},{1,5},{2,6},{3,7},{4,0},{5,1},{6,2},{7,3},{8,12},{9,13},{10,... | collective-permute-start | bytes 393224 | tf_op jit(solution)/shard_map/ppermute | solution.py:89
  18.8 0.2 collective-permute-start.4
  19.0 3.7 %collective-permute-done.2 = f32[2,128,128]{2,1,0:T(8,128)S(1)} collective-permute-done((f32[2,128,128]{2,1,0:T(8,128)S(1)}, f32[2,128,128]{2,1,0:T(8,128)S(1)}, u32[]{:S(2)}, u32[]{:S(2)}) %collective-permute-start.2) | collective-permute-done | bytes 131104 | tf_op jit(solution)/shard_map/ppermute | solution.py:89
  22.7 1.5 %collective-permute-done.3 = f32[2,128,128]{2,1,0:T(8,128)S(1)} collective-permute-done((f32[2,128,128]{2,1,0:T(8,128)S(1)}, f32[2,128,128]{2,1,0:T(8,128)S(1)}, u32[]{:S(2)}, u32[]{:S(2)}) %collective-permute-start.3) | collective-permute-done | bytes 131104 | tf_op jit(solution)/shard_map/ppermute | solution.py:89
  24.3 0.0 collective-permute-done.4
  24.3 2.7 %collective-permute-start.5 = (f32[1,128,128]{2,1,0:T(8,128)S(1)}, f32[1,128,128]{2,1,0:T(8,128)S(1)}, u32[]{:S(2)}, u32[]{:S(2)}) collective-permute-start(f32[1,128,128]{2,1,0:T(8,128)S(1)} %slice.47), channel_id=1, source_target_pairs={{0,8},{1,9},{2,10},{3,11},{4,12},{5,13},{6,14},{7,15},{8,0},{9,1},... | collective-permute-start | bytes 196616 | tf_op jit(solution)/shard_map/ppermute | solution.py:89
  27.0 2.6 %collective-permute-done.5 = f32[1,128,128]{2,1,0:T(8,128)S(1)} collective-permute-done((f32[1,128,128]{2,1,0:T(8,128)S(1)}, f32[1,128,128]{2,1,0:T(8,128)S(1)}, u32[]{:S(2)}, u32[]{:S(2)}) %collective-permute-start.5) | collective-permute-done | bytes 65568 | tf_op jit(solution)/shard_map/ppermute | solution.py:89
  29.6 0.1 collective-permute-start.6
  29.7 1.2 %collective-permute-done.6 = f32[128,128]{1,0:T(8,128)S(1)} collective-permute-done((f32[128,128]{1,0:T(8,128)S(1)}, f32[128,128]{1,0:T(8,128)S(1)}, u32[]{:S(2)}, u32[]{:S(2)}) %collective-permute-start.6) | collective-permute-done | bytes 65568 | tf_op jit(solution)/shard_map/ppermute | solution.py:94
  30.9 0.7 %pad_maximum_fusion = f32[2,128,128]{2,1,0:T(8,128)} fusion(f32[1,128,128]{2,1,0:T(8,128)S(1)} %get-tuple-element.9, f32[1,128,128]{2,1,0:T(8,128)S(1)} %get-tuple-element.8), kind=kLoop, calls=%fused_computation.6 | loop fusion | flops 32768 | bytes 262144 | tf_op jit(solution)/shard_map/stack | solution.py:95
  (6 shorter events, 0.1 us)
Async XLA Ops:
  2.0 2.8 %collective-permute-start = (f32[16,1,128,128]{3,2,1,0:T(8,128)S(1)}, f32[16,1,128,128]{3,2,1,0:T(8,128)S(1)}, u32[]{:S(2)}, u32[]{:S(2)}) collective-permute-start(f32[16,1,128,128]{3,2,1,0:T(8,128)S(1)} %shard_map.29), channel_id=1, source_target_pairs={{0,16},{16,0},{1,17},{17,1},{2,18},{18,2},{3,19},{19,3},{4,20},{20... | collective-permute-start | bytes 3145736 | tf_op jit(solution)/shard_map/ppermute | solution.py:71
  5.1 10.1 %collective-permute-start.1 = (f32[8,128,128]{2,1,0:T(8,128)S(1)}, f32[8,128,128]{2,1,0:T(8,128)S(1)}, u32[]{:S(2)}, u32[]{:S(2)}) collective-permute-start(f32[8,128,128]{2,1,0:T(8,128)S(1)} %slice_bitcast_fusion), channel_id=1, source_target_pairs={{0,1},{1,0},{2,3},{3,2},{4,5},{5,4},{6,7},{7,6},{8,9},{9,8},{10,11... | collective-permute-start | bytes 1572872 | tf_op jit(solution)/shard_map/ppermute | solution.py:89
  15.3 7.5 %collective-permute-start.2 = (f32[2,128,128]{2,1,0:T(8,128)S(1)}, f32[2,128,128]{2,1,0:T(8,128)S(1)}, u32[]{:S(2)}, u32[]{:S(2)}) collective-permute-start(f32[2,128,128]{2,1,0:T(8,128)S(1)} %get-tuple-element.5), channel_id=1, source_target_pairs={{0,6},{1,7},{2,4},{3,5},{4,2},{5,3},{6,0},{7,1},{8,14},{9,15},{10,... | collective-permute-start | bytes 393224 | tf_op jit(solution)/shard_map/ppermute | solution.py:89
  18.4 5.9 %collective-permute-start.3 = (f32[2,128,128]{2,1,0:T(8,128)S(1)}, f32[2,128,128]{2,1,0:T(8,128)S(1)}, u32[]{:S(2)}, u32[]{:S(2)}) collective-permute-start(f32[2,128,128]{2,1,0:T(8,128)S(1)} %get-tuple-element.7), channel_id=1, source_target_pairs={{0,4},{1,5},{2,6},{3,7},{4,0},{5,1},{6,2},{7,3},{8,12},{9,13},{10,... | collective-permute-start | bytes 393224 | tf_op jit(solution)/shard_map/ppermute | solution.py:89
  18.8 5.4 %collective-permute-start.4 = (f32[2,128,128]{2,1,0:T(8,128)S(1)}, f32[2,128,128]{2,1,0:T(8,128)S(1)}, u32[]{:S(2)}, u32[]{:S(2)}) collective-permute-start(f32[2,128,128]{2,1,0:T(8,128)S(1)} %get-tuple-element.6), channel_id=1, source_target_pairs={{0,2},{1,3},{2,0},{3,1},{4,6},{5,7},{6,4},{7,5},{8,10},{9,11},{10,... | collective-permute-start | bytes 393224 | tf_op jit(solution)/shard_map/ppermute | solution.py:89
  24.3 5.2 %collective-permute-start.5 = (f32[1,128,128]{2,1,0:T(8,128)S(1)}, f32[1,128,128]{2,1,0:T(8,128)S(1)}, u32[]{:S(2)}, u32[]{:S(2)}) collective-permute-start(f32[1,128,128]{2,1,0:T(8,128)S(1)} %slice.47), channel_id=1, source_target_pairs={{0,8},{1,9},{2,10},{3,11},{4,12},{5,13},{6,14},{7,15},{8,0},{9,1},... | collective-permute-start | bytes 196616 | tf_op jit(solution)/shard_map/ppermute | solution.py:89
  29.6 1.3 %collective-permute-start.6 = (f32[128,128]{1,0:T(8,128)S(1)}, f32[128,128]{1,0:T(8,128)S(1)}, u32[]{:S(2)}, u32[]{:S(2)}) collective-permute-start(f32[128,128]{1,0:T(8,128)S(1)} %fusion.3), channel_id=1, source_target_pairs={{0,16},{16,0},{1,17},{17,1},{2,18},{18,2},{3,19},{19,3},{4,20},{20... | collective-permute-start | bytes 196616 | tf_op jit(solution)/shard_map/ppermute | solution.py:94

commit v2 on v1

--- a/solution.py
+++ b/solution.py
@@ -30,7 +30,8 @@
 
 
 def scaled_half(source, scale, half, order, shard, offsets):
-    blocks, inner, _, rows, lanes = source.shape
+    _, inner, _, rows, lanes = source.shape
+    blocks = len(offsets[0])
 
     def kernel(half_ref, order_ref, shard_ref, scale_ref, source_ref, out_ref, sems):
         copies = []
@@ -60,24 +61,36 @@
     snap_bits = snaps.bit_length() - 1
     phases = phases_of(bits)
     offsets = [offsets_of(p) for p in phases]
+    first = [order[0][0] for order in phases]
 
     def per_device(snapshots, coefficients):
         params = snapshots.shape[1]
         rows = params // shards // snaps // LANES
         snap, shard = lax.axis_index("snap"), lax.axis_index("shard")
         source = snapshots.reshape(shards, -1, 2, rows, LANES)
-        mine = snap & 1
-        send = scaled_half(source, coefficients, 1 - mine, 1 - mine, shard, offsets)
-        got = lax.ppermute(send, "snap", [(s, s ^ 1) for s in range(snaps)])
-        part = scaled_half(source, coefficients, mine, mine, shard, offsets) + got
-        for bit in range(1, snap_bits):
-            mine = (snap >> bit) & 1
-            part = part.reshape(shards, -1, 2, rows, LANES)
-            send = lax.dynamic_index_in_dim(part, 1 - mine, 2, keepdims=False)
-            keep = lax.dynamic_index_in_dim(part, mine, 2, keepdims=False)
-            part = keep + lax.ppermute(send, "snap", [(s, s ^ (1 << bit)) for s in range(snaps)])
-        part = part.reshape(shards, rows, LANES)
-        for even, odd in zip(*phases):
+        def snap_sum(scale, places):
+            mine = snap & 1
+            send = scaled_half(source, scale, 1 - mine, 1 - mine, shard, places)
+            got = lax.ppermute(send, "snap", [(s, s ^ 1) for s in range(snaps)])
+            part = scaled_half(source, scale, mine, mine, shard, places) + got
+            for bit in range(1, snap_bits):
+                mine = (snap >> bit) & 1
+                part = part.reshape(len(places[0]), -1, 2, rows, LANES)
+                send = lax.dynamic_index_in_dim(part, 1 - mine, 2, keepdims=False)
+                keep = lax.dynamic_index_in_dim(part, mine, 2, keepdims=False)
+                part = keep + lax.ppermute(send, "snap", [(s, s ^ (1 << bit)) for s in range(snaps)])
+            return part.reshape(-1, rows, LANES)
+
+        half = shards // 2
+        sent = snap_sum(coefficients, [order[half:] for order in offsets])
+        scale, sent = lax.optimization_barrier((coefficients, sent))
+        pairs = [
+            (s * shards + d, s * shards + (d ^ first[s & 1]))
+            for s in range(snaps) for d in range(shards)
+        ]
+        came = lax.ppermute(sent, ("snap", "shard"), pairs)
+        part = snap_sum(scale, [order[:half] for order in offsets]) + came
+        for even, odd in zip(*(order[1:] for order in phases)):
             masks = list(zip(span(even), span(odd)))
             part = part.reshape(len(masks), -1, rows, LANES)
             total = part[0]

time: 31.8 us -> 31.7 us (level)
  waiting for transfers between devices: 17.1 us -> 15 us
  Pallas kernels: 2.76 us -> 4.54 us
    ppermute x5 -> x4, waiting for transfers between devices: 15 us -> 7.71 us  [per_device(): total = total + lax.ppermute(part[k], ('snap', 'shard'), pairs)]
    ppermute x1 -> x3, waiting for transfers between devices: 0.9 us -> 6.01 us  [the longest x1 6.01 us: per_device(): came = lax.ppermute(sent, ('snap', 'shard'), pairs)]
    ppermute x1 -> x3, starting transfers between devices: 0.56 us -> 3.67 us  [the longest x1 3.02 us: per_device(): came = lax.ppermute(sent, ('snap', 'shard'), pairs)]
    ppermute x5 -> x4, starting transfers between devices: 9.34 us -> 6.42 us  [per_device(): total = total + lax.ppermute(part[k], ('snap', 'shard'), pairs)]
    pallas_call x2 -> x4, Pallas kernels: 2.76 us -> 4.54 us  [scaled_half(): pl.pallas_call(kernel, out_shape=pltpu.VMEM((blocks, inner, rows, lanes),...]
  transfers between devices with their start and end apart: 7 -> 8, of which waited for: 6 -> 5; matrix products, arithmetic and copies ran while one was open for 0% -> 0% of each run, Pallas kernels for 4% -> 11%
where the time goes in v2:
time: 31.7 us; the launch traced here: 31.3 us
  waiting for transfers between devices  15 us (47%)
  starting transfers between devices  10.2 us (32%)
  Pallas kernels  4.54 us (14%)
  other arithmetic  0.86 us (3%)
  between operations  0.75 us (2%)
    ppermute x4, waiting for transfers between devices, per_device(): total = total + lax.ppermute(part[k], ('snap', 'shard'), pairs)  7.71 us
    ppermute x4, starting transfers between devices, per_device(): total = total + lax.ppermute(part[k], ('snap', 'shard'), pairs)  6.42 us
    ppermute x1, waiting for transfers between devices, per_device(): came = lax.ppermute(sent, ('snap', 'shard'), pairs)  6.01 us
    pallas_call x4, Pallas kernels, scaled_half(): pl.pallas_call(kernel, out_shape=pltpu.VMEM((blocks, inner, rows, lanes),...  4.54 us
    ppermute x1, starting transfers between devices, per_device(): came = lax.ppermute(sent, ('snap', 'shard'), pairs)  3.02 us
    ppermute x1, waiting for transfers between devices, per_device(): got = lax.ppermute(own, 'snap', [(s, s ^ 1 << bit) for s in range(snaps)])  1.24 us
    another operation x2, other arithmetic, per_device(): jnp.stack([jnp.where(mine == 0, own, got), jnp.where(mine == 0, got, own)])  0.68 us
    ppermute x2, starting transfers between devices, snap_sum(): got = lax.ppermute(send, 'snap', [(s, s ^ 1) for s in range(snaps)])  0.65 us
  transfers between devices with their start and end apart: 8, of which 5 were waited for; matrix products, arithmetic and copies ran while one was open for 0% of the time, Pallas kernels for 11%

profile of v2, /device:TPU:0, one launch (start us, length us, event | category | flops | bytes accessed | tf_op | source)
XLA Modules:
  0.0 31.3 jit_solution(3271765694903099861)
XLA Ops:
  0.7 1.1 %shard_map.29 = f32[8,1,128,128]{3,2,1,0:T(8,128)S(1)} custom-call(s32[1]{0:T(128)} %bitcast.4.half_ref.order_ref, s32[1]{0:T(128)} %bitcast.4.half_ref.order_ref, s32[1]{0:T(128)} %bitcast.1.shard_ref, f32[1]{0:T(128)S(6)} %copy.5.scale_ref, f32[16,1,2,128,128]{4,3,2,1,0:T(8,128)} %bitcast.21), custom_call_target="tpu_custom_call" | custom-call | tf_op jit(solution)/shard_map/pallas_call | solution.py:49
  1.8 0.6 %collective-permute-start = (f32[8,1,128,128]{3,2,0,1:T(8,128)S(1)}, f32[8,1,128,128]{3,2,0,1:T(8,128)S(1)}, u32[]{:S(2)}, u32[]{:S(2)}) collective-permute-start(f32[8,1,128,128]{3,2,0,1:T(8,128)S(1)} %bitcast.20), channel_id=1, source_target_pairs={{0,16},{16,0},{1,17},{17,1},{2,18},{18,2},{3,19},{19,3},{4,20},{20... | collective-permute-start | bytes 1572872 | tf_op jit(solution)/shard_map/ppermute | solution.py:74
  2.4 1.1 %shard_map.31 = f32[8,1,128,128]{3,2,1,0:T(8,128)S(1)} custom-call(s32[1]{0:T(128)} %bitcast.4.half_ref.order_ref, s32[1]{0:T(128)} %bitcast.4.half_ref.order_ref, s32[1]{0:T(128)} %bitcast.1.shard_ref, f32[1]{0:T(128)S(6)} %copy.5.scale_ref, f32[16,1,2,128,128]{4,3,2,1,0:T(8,128)} %bitcast.22), custom_call_target="tpu_custom_call" | custom-call | tf_op jit(solution)/shard_map/pallas_call | solution.py:49
  3.5 0.1 collective-permute-start.1
  3.6 1.1 %shard_map.28 = f32[8,1,128,128]{3,2,1,0:T(8,128)S(1)} custom-call(s32[1]{0:T(128)} %bitcast.half_ref.order_ref, s32[1]{0:T(128)} %bitcast.half_ref.order_ref, s32[1]{0:T(128)} %bitcast.1.shard_ref, f32[1]{0:T(128)S(6)} %copy.5.scale_ref, f32[16,1,2,128,128]{4,3,2,1,0:T(8,128)} %bitcast.23), custom_call_target="tpu_custom_call" | custom-call | tf_op jit(solution)/shard_map/pallas_call | solution.py:49
  4.7 0.0 collective-permute-done
  4.7 0.1 fusion
  4.8 3.0 %collective-permute-start.2 = (f32[8,128,128]{2,1,0:T(8,128)S(1)}, f32[8,128,128]{2,1,0:T(8,128)S(1)}, u32[]{:S(2)}, u32[]{:S(2)}) collective-permute-start(f32[8,128,128]{2,1,0:T(8,128)S(1)} %fusion), channel_id=1, source_target_pairs={{0,1},{1,0},{2,3},{3,2},{4,5},{5,4},{6,7},{7,6},{8,9},{9,8},{10,11... | collective-permute-start | bytes 1572872 | tf_op jit(solution)/shard_map/ppermute | solution.py:91
  7.8 1.1 %shard_map.30 = f32[8,1,128,128]{3,2,1,0:T(8,128)S(1)} custom-call(s32[1]{0:T(128)} %bitcast.half_ref.order_ref, s32[1]{0:T(128)} %bitcast.half_ref.order_ref, s32[1]{0:T(128)} %bitcast.1.shard_ref, f32[1]{0:T(128)S(6)} %copy.5.scale_ref, f32[16,1,2,128,128]{4,3,2,1,0:T(8,128)} %bitcast.24), custom_call_target="tpu_custom_call" | custom-call | tf_op jit(solution)/shard_map/pallas_call | solution.py:49
  9.0 0.0 collective-permute-done.1
  9.0 6.0 %collective-permute-done.2 = f32[8,128,128]{2,1,0:T(8,128)S(1)} collective-permute-done((f32[8,128,128]{2,1,0:T(8,128)S(1)}, f32[8,128,128]{2,1,0:T(8,128)S(1)}, u32[]{:S(2)}, u32[]{:S(2)}) %collective-permute-start.2) | collective-permute-done | bytes 524320 | tf_op jit(solution)/shard_map/ppermute | solution.py:91
  15.0 0.1 bitcast_add_fusion
  15.1 3.1 %collective-permute-start.3 = (f32[2,128,128]{2,1,0:T(8,128)S(1)}, f32[2,128,128]{2,1,0:T(8,128)S(1)}, u32[]{:S(2)}, u32[]{:S(2)}) collective-permute-start(f32[2,128,128]{2,1,0:T(8,128)S(1)} %get-tuple-element.9), channel_id=1, source_target_pairs={{0,6},{1,7},{2,4},{3,5},{4,2},{5,3},{6,0},{7,1},{8,14},{9,15},{10,... | collective-permute-start | bytes 393224 | tf_op jit(solution)/shard_map/ppermute | solution.py:102
  18.2 0.4 %collective-permute-start.4 = (f32[2,128,128]{2,1,0:T(8,128)S(1)}, f32[2,128,128]{2,1,0:T(8,128)S(1)}, u32[]{:S(2)}, u32[]{:S(2)}) collective-permute-start(f32[2,128,128]{2,1,0:T(8,128)S(1)} %get-tuple-element.11), channel_id=1, source_target_pairs={{0,4},{1,5},{2,6},{3,7},{4,0},{5,1},{6,2},{7,3},{8,12},{9,13},{10,... | collective-permute-start | bytes 393224 | tf_op jit(solution)/shard_map/ppermute | solution.py:102
  18.7 0.2 collective-permute-start.5
  18.9 3.7 %collective-permute-done.3 = f32[2,128,128]{2,1,0:T(8,128)S(1)} collective-permute-done((f32[2,128,128]{2,1,0:T(8,128)S(1)}, f32[2,128,128]{2,1,0:T(8,128)S(1)}, u32[]{:S(2)}, u32[]{:S(2)}) %collective-permute-start.3) | collective-permute-done | bytes 131104 | tf_op jit(solution)/shard_map/ppermute | solution.py:102
  22.6 1.4 %collective-permute-done.4 = f32[2,128,128]{2,1,0:T(8,128)S(1)} collective-permute-done((f32[2,128,128]{2,1,0:T(8,128)S(1)}, f32[2,128,128]{2,1,0:T(8,128)S(1)}, u32[]{:S(2)}, u32[]{:S(2)}) %collective-permute-start.4) | collective-permute-done | bytes 131104 | tf_op jit(solution)/shard_map/ppermute | solution.py:102
  24.0 0.0 collective-permute-done.5
  24.1 2.7 %collective-permute-start.6 = (f32[1,128,128]{2,1,0:T(8,128)S(1)}, f32[1,128,128]{2,1,0:T(8,128)S(1)}, u32[]{:S(2)}, u32[]{:S(2)}) collective-permute-start(f32[1,128,128]{2,1,0:T(8,128)S(1)} %slice.35), channel_id=1, source_target_pairs={{0,8},{1,9},{2,10},{3,11},{4,12},{5,13},{6,14},{7,15},{8,0},{9,1},... | collective-permute-start | bytes 196616 | tf_op jit(solution)/shard_map/ppermute | solution.py:102
  26.7 2.6 %collective-permute-done.6 = f32[1,128,128]{2,1,0:T(8,128)S(1)} collective-permute-done((f32[1,128,128]{2,1,0:T(8,128)S(1)}, f32[1,128,128]{2,1,0:T(8,128)S(1)}, u32[]{:S(2)}, u32[]{:S(2)}) %collective-permute-start.6) | collective-permute-done | bytes 65568 | tf_op jit(solution)/shard_map/ppermute | solution.py:102
  29.3 0.1 collective-permute-start.7
  29.4 1.2 %collective-permute-done.7 = f32[128,128]{1,0:T(8,128)S(1)} collective-permute-done((f32[128,128]{1,0:T(8,128)S(1)}, f32[128,128]{1,0:T(8,128)S(1)}, u32[]{:S(2)}, u32[]{:S(2)}) %collective-permute-start.7) | collective-permute-done | bytes 65568 | tf_op jit(solution)/shard_map/ppermute | solution.py:107
  30.7 0.7 %pad_maximum_fusion = f32[2,128,128]{2,1,0:T(8,128)} fusion(f32[1,128,128]{2,1,0:T(8,128)S(1)} %get-tuple-element.13, f32[1,128,128]{2,1,0:T(8,128)S(1)} %get-tuple-element.12), kind=kLoop, calls=%fused_computation.6 | loop fusion | flops 32768 | bytes 262144 | tf_op jit(solution)/shard_map/stack | solution.py:108
  (5 shorter events, 0.1 us)
Async XLA Ops:
  1.8 2.9 %collective-permute-start = (f32[8,1,128,128]{3,2,0,1:T(8,128)S(1)}, f32[8,1,128,128]{3,2,0,1:T(8,128)S(1)}, u32[]{:S(2)}, u32[]{:S(2)}) collective-permute-start(f32[8,1,128,128]{3,2,0,1:T(8,128)S(1)} %bitcast.20), channel_id=1, source_target_pairs={{0,16},{16,0},{1,17},{17,1},{2,18},{18,2},{3,19},{19,3},{4,20},{20... | collective-permute-start | bytes 1572872 | tf_op jit(solution)/shard_map/ppermute | solution.py:74
  3.5 5.5 %collective-permute-start.1 = (f32[8,1,128,128]{3,2,1,0:T(8,128)S(1)}, f32[8,1,128,128]{3,2,1,0:T(8,128)S(1)}, u32[]{:S(2)}, u32[]{:S(2)}) collective-permute-start(f32[8,1,128,128]{3,2,1,0:T(8,128)S(1)} %shard_map.31), channel_id=1, source_target_pairs={{0,16},{16,0},{1,17},{17,1},{2,18},{18,2},{3,19},{19,3},{4,20},{20... | collective-permute-start | bytes 1572872 | tf_op jit(solution)/shard_map/ppermute | solution.py:74
  4.8 10.2 %collective-permute-start.2 = (f32[8,128,128]{2,1,0:T(8,128)S(1)}, f32[8,128,128]{2,1,0:T(8,128)S(1)}, u32[]{:S(2)}, u32[]{:S(2)}) collective-permute-start(f32[8,128,128]{2,1,0:T(8,128)S(1)} %fusion), channel_id=1, source_target_pairs={{0,1},{1,0},{2,3},{3,2},{4,5},{5,4},{6,7},{7,6},{8,9},{9,8},{10,11... | collective-permute-start | bytes 1572872 | tf_op jit(solution)/shard_map/ppermute | solution.py:91
  15.1 7.5 %collective-permute-start.3 = (f32[2,128,128]{2,1,0:T(8,128)S(1)}, f32[2,128,128]{2,1,0:T(8,128)S(1)}, u32[]{:S(2)}, u32[]{:S(2)}) collective-permute-start(f32[2,128,128]{2,1,0:T(8,128)S(1)} %get-tuple-element.9), channel_id=1, source_target_pairs={{0,6},{1,7},{2,4},{3,5},{4,2},{5,3},{6,0},{7,1},{8,14},{9,15},{10,... | collective-permute-start | bytes 393224 | tf_op jit(solution)/shard_map/ppermute | solution.py:102
  18.2 5.8 %collective-permute-start.4 = (f32[2,128,128]{2,1,0:T(8,128)S(1)}, f32[2,128,128]{2,1,0:T(8,128)S(1)}, u32[]{:S(2)}, u32[]{:S(2)}) collective-permute-start(f32[2,128,128]{2,1,0:T(8,128)S(1)} %get-tuple-element.11), channel_id=1, source_target_pairs={{0,4},{1,5},{2,6},{3,7},{4,0},{5,1},{6,2},{7,3},{8,12},{9,13},{10,... | collective-permute-start | bytes 393224 | tf_op jit(solution)/shard_map/ppermute | solution.py:102
  18.7 5.3 %collective-permute-start.5 = (f32[2,128,128]{2,1,0:T(8,128)S(1)}, f32[2,128,128]{2,1,0:T(8,128)S(1)}, u32[]{:S(2)}, u32[]{:S(2)}) collective-permute-start(f32[2,128,128]{2,1,0:T(8,128)S(1)} %get-tuple-element.10), channel_id=1, source_target_pairs={{0,2},{1,3},{2,0},{3,1},{4,6},{5,7},{6,4},{7,5},{8,10},{9,11},{10,... | collective-permute-start | bytes 393224 | tf_op jit(solution)/shard_map/ppermute | solution.py:102
  24.1 5.2 %collective-permute-start.6 = (f32[1,128,128]{2,1,0:T(8,128)S(1)}, f32[1,128,128]{2,1,0:T(8,128)S(1)}, u32[]{:S(2)}, u32[]{:S(2)}) collective-permute-start(f32[1,128,128]{2,1,0:T(8,128)S(1)} %slice.35), channel_id=1, source_target_pairs={{0,8},{1,9},{2,10},{3,11},{4,12},{5,13},{6,14},{7,15},{8,0},{9,1},... | collective-permute-start | bytes 196616 | tf_op jit(solution)/shard_map/ppermute | solution.py:102
  29.3 1.3 %collective-permute-start.7 = (f32[128,128]{1,0:T(8,128)S(1)}, f32[128,128]{1,0:T(8,128)S(1)}, u32[]{:S(2)}, u32[]{:S(2)}) collective-permute-start(f32[128,128]{1,0:T(8,128)S(1)} %fusion.3), channel_id=1, source_target_pairs={{0,16},{16,0},{1,17},{17,1},{2,18},{18,2},{3,19},{19,3},{4,20},{20... | collective-permute-start | bytes 196616 | tf_op jit(solution)/shard_map/ppermute | solution.py:107
